TPU v7x, 32 devices: a whole 2x2x4 slice. The times are simulated.
32 devices in a mesh: groups: 2 (over y), dp: 4 (over z), section: 2 (over x), tensor: 2 (over core).
Axes of the slice: x: 2, y: 2, z: 4, core: 2. Of those that a mesh axis runs over, the one named last changes fastest.
Arguments:
- hidden: bfloat16 [128, 8, 5120], P(('groups', 'dp')), parts along dimension 0, may hold values from -6 to 6
- unembed: bfloat16 [128, 8, 5120], P(('groups', 'dp')), parts along dimension 0, may hold values from -0.02734375 to 0.02734375
- value_proj: bfloat16 [2, 5120, 512], P('section', 'dp', 'tensor'), may hold values from -0.078125 to 0.078125
- output_proj: bfloat16 [2, 512, 5120], P('section', 'tensor', 'dp'), may hold values from -0.125 to 0.125
- norm_gains: float32 [2, 5120], P('section'), may hold values from 0.1 to 1.9
- survive: int32 [8], P(('groups', 'dp')), parts along dimension 0, may hold values from 0 to 1, as said below
- lengths: int32 [128], P(('groups', 'dp')), parts along dimension 0, may hold values from 1 to 8
- assign: int32 [128], P(('groups', 'dp')), parts along dimension 0, may hold values from 0 to 16, as said below
- advantage: float32 [128], P(('groups', 'dp')), parts along dimension 0, may hold values from -4 to 4
- reference_logit: float32 [128, 8], P(('groups', 'dp')), parts along dimension 0, may hold values from -4 to 4
- recorded_gap: float32 [128, 8], P(('groups', 'dp')), parts along dimension 0, may hold values from -2 to 2
Outputs:
- grad_value: float32 [4, 5120, 512], P(('groups', 'section'), 'dp', 'tensor'), parts along dimension 0
- grad_output: float32 [4, 512, 5120], P(('groups', 'section'), 'tensor', 'dp'), parts along dimension 0
There are 2 independent parts, one for each index of `groups`. A program takes and returns all parts, laid end to end along the dimension named above; an argument that names none is the same for every part. Nothing has to cross between parts.
Inputs may be any that keep to these rules, and one draw needn't show every extreme that they name: `survive`: 1 where the group of 16 responses is kept, 0 where it is dropped; in every draw all groups of some dp index are kept. `assign`: the 16 slots of a dp index list the local positions (0 to 15) of the responses of its kept groups, each exactly once, then hold 16 in every other slot.
All inputs are finite; a program needn't handle non-finite values.
Results may differ from a plain program's by a relative error of at most 0.029.
Values may be sent and summed in bfloat16 or wider, within the bound.
A program may use at most 64 MiB of HBM per device.

v0:
```python
import math
import jax
import jax.numpy as jnp
from jax import lax
from jax.sharding import PartitionSpec as P

GROUP = 16
MB_RESP = 8
eps_norm = 1e-06
loss_scale = 4096.0
clip_high = math.log(1.28)
clip_low = math.log(0.8)


def from_behind(block, axis, distance):
    devices = range(lax.axis_size(axis))
    route = [(i - distance, i) for i in devices if i - distance in devices]
    return lax.ppermute(block, axis, route)


def norm_forward(row_block, norm_gain):
    values = row_block.astype(jnp.float32)
    inverse = lax.rsqrt(jnp.mean(values * values, axis=-1, keepdims=True) + eps_norm)
    return (values, inverse, (values * inverse * norm_gain).astype(jnp.bfloat16))


def norm_backward(values, inverse, norm_gain, upstream):
    scaled = upstream * norm_gain
    inner_sum = jnp.sum(scaled * values, axis=-1, keepdims=True) / values.shape[-1]
    return inverse * scaled - values * (inverse * inverse * inverse) * inner_sum


def contract_last(left_rows, right_rows):
    return lax.dot_general(
        left_rows, right_rows, (((1,), (1,)), ((), ())), preferred_element_type=jnp.float32
    )


def contract_first(left_rows, right_rows):
    return lax.dot_general(
        left_rows, right_rows, (((0,), (0,)), ((), ())), preferred_element_type=jnp.float32
    )


def take_slot(slot_store, slot_index):
    return lax.dynamic_index_in_dim(slot_store, slot_index, 0, keepdims=False)


def put_slot(slot_store, new_value, slot_index, active):
    previous = take_slot(slot_store, slot_index)
    return lax.dynamic_update_index_in_dim(
        slot_store, jnp.where(active, new_value, previous), slot_index, 0
    )


def local(
    hidden,
    unembed,
    value_proj,
    output_proj,
    norm_gains,
    survive,
    lengths,
    assign,
    advantage,
    reference_logit,
    recorded_gap,
):
    resp_count = hidden.shape[0]
    positions = hidden.shape[1]
    model_width = hidden.shape[2]
    half_value = value_proj.shape[2]
    micro_count = resp_count // MB_RESP
    row_count = MB_RESP * positions
    section_count = lax.axis_size("section")
    section_index = lax.axis_index("section")
    is_last = section_index == section_count - 1
    norm_gain = norm_gains[0]
    alive_mask = jnp.repeat(survive, GROUP)
    local_count = jnp.sum((alive_mask * lengths).astype(jnp.float32))
    gathered_value, gathered_output = (
        lax.all_gather(value_proj, "dp", axis=1, tiled=True),
        lax.all_gather(output_proj, "dp", axis=2, tiled=True),
    )
    w_first = gathered_value[0]
    w_second = gathered_output[0]

    def pick(array):
        return jnp.take(array, assign, axis=0, mode="fill", fill_value=0)

    slot_hidden = pick(hidden).reshape(micro_count, row_count, model_width)
    slot_unembed = pick(unembed).reshape(micro_count, row_count, model_width)
    position_index = lax.broadcasted_iota(jnp.int32, (resp_count, positions), 1)
    live_mask = (position_index < pick(lengths)[:, None]).astype(jnp.float32)
    advantages = jnp.broadcast_to(pick(advantage)[:, None], (resp_count, positions))
    gap_rows = pick(recorded_gap)
    clipped = (advantages > 0) & (gap_rows > clip_high) | (advantages < 0) & (gap_rows < clip_low)
    kept_mask = 1.0 - clipped.astype(jnp.float32)
    weight_rows = (-loss_scale * advantages * kept_mask * live_mask).reshape(micro_count, row_count)
    logit_base = pick(reference_logit).reshape(micro_count, row_count)
    step_count = micro_count + section_count - 1
    store_in = jnp.zeros((micro_count, row_count, model_width), jnp.bfloat16)
    store_normed = jnp.zeros((micro_count, row_count, model_width), jnp.bfloat16)
    store_projected = jnp.zeros((micro_count, row_count, half_value), jnp.bfloat16)
    store_out = jnp.zeros((micro_count, row_count, model_width), jnp.bfloat16)
    arriving = jnp.zeros((row_count, model_width), jnp.bfloat16)
    for step_index in range(step_count):
        micro_index = step_index - section_index
        active = (micro_index >= 0) & (micro_index < micro_count)
        clamped = jnp.clip(micro_index, 0, micro_count - 1)
        entering = jnp.where(section_index == 0, take_slot(slot_hidden, clamped), arriving)
        values, inverse, normed = norm_forward(entering, norm_gain)
        projected = jnp.dot(normed, w_first, preferred_element_type=jnp.float32).astype(
            jnp.bfloat16
        )
        partial_out = jnp.dot(projected, w_second, preferred_element_type=jnp.float32)
        mixed_sum = lax.psum(partial_out.astype(jnp.bfloat16), "tensor").astype(jnp.float32)
        leaving = (values + mixed_sum).astype(jnp.bfloat16)
        store_in = put_slot(store_in, entering, clamped, active)
        store_normed = put_slot(store_normed, normed, clamped, active)
        store_projected = put_slot(store_projected, projected, clamped, active)
        store_out = put_slot(store_out, leaving, clamped, active)
        arriving = from_behind(leaving, "section", 1)
    store_upstream = jnp.zeros((micro_count, row_count, model_width), jnp.bfloat16)
    store_grad_value = jnp.zeros((micro_count, row_count, half_value), jnp.bfloat16)
    arriving = jnp.zeros((row_count, model_width), jnp.bfloat16)
    for step_index in range(step_count):
        micro_index = step_index - (section_count - 1 - section_index)
        active = (micro_index >= 0) & (micro_index < micro_count)
        clamped = jnp.clip(micro_index, 0, micro_count - 1)
        top_rows = take_slot(store_out, clamped).astype(jnp.float32)
        unembed_rows = take_slot(slot_unembed, clamped).astype(jnp.float32)
        logit = jnp.sum(top_rows * unembed_rows, axis=-1)
        seed_rows = take_slot(weight_rows, clamped) * jnp.exp(
            logit - take_slot(logit_base, clamped)
        )
        start_grad = (seed_rows[:, None] * unembed_rows).astype(jnp.bfloat16)
        upstream = jnp.where(is_last, start_grad, arriving)
        entering = take_slot(store_in, clamped)
        normed = take_slot(store_normed, clamped)
        projected = take_slot(store_projected, clamped)
        grad_projected = contract_last(upstream, w_second).astype(jnp.bfloat16)
        partial_norm = contract_last(grad_projected, w_first)
        grad_normed = lax.psum(partial_norm.astype(jnp.bfloat16), "tensor").astype(jnp.float32)
        values, inverse, unused_normed = norm_forward(entering, norm_gain)
        grad_entering = (
            upstream.astype(jnp.float32) + norm_backward(values, inverse, norm_gain, grad_normed)
        ).astype(jnp.bfloat16)
        store_upstream = put_slot(store_upstream, upstream, clamped, active)
        store_grad_value = put_slot(store_grad_value, grad_projected, clamped, active)
        arriving = from_behind(grad_entering, "section", -1)
    flat_normed = store_normed.reshape(micro_count * row_count, model_width)
    flat_upstream = store_upstream.reshape(micro_count * row_count, model_width)
    flat_grad_value = store_grad_value.reshape(micro_count * row_count, half_value)
    flat_projected = store_projected.reshape(micro_count * row_count, half_value)
    reduced = lax.psum_scatter(
        jnp.concatenate(
            [
                contract_first(flat_normed, flat_grad_value),
                contract_first(flat_upstream, flat_projected),
            ],
            axis=1,
        ).astype(jnp.bfloat16),
        "dp",
        scatter_dimension=0,
        tiled=True,
    ).astype(jnp.float32)
    token_total = lax.psum(local_count, "dp")
    scaled_grads = reduced / token_total
    grad_value = scaled_grads[:, :half_value][None]
    grad_output = scaled_grads[:, half_value:].T[None]
    return (grad_value, grad_output)


def solution(mesh):
    placed = (
        P(("groups", "dp"), None, None),
        P(("groups", "dp"), None, None),
        P("section", "dp", "tensor"),
        P("section", "tensor", "dp"),
        P("section", None),
        P(("groups", "dp")),
        P(("groups", "dp")),
        P(("groups", "dp")),
        P(("groups", "dp")),
        P(("groups", "dp"), None),
        P(("groups", "dp"), None),
    )
    return jax.shard_map(
        local,
        mesh=mesh,
        in_specs=placed,
        out_specs=(
            P(("groups", "section"), "dp", "tensor"),
            P(("groups", "section"), "tensor", "dp"),
        ),
        check_vma=False,
    )
```

profile of v0, /device:TPU:0, one launch (start us, length us, event | category | flops | bytes accessed | tf_op | source)
XLA Modules:
  0.0 449.3 jit_solution(629598408572374933)
XLA Ops:
  18.2 48.9 %all-gather.3.cloned.1.call-done = bf16[1,5120,256]{2,1,0:T(8,128)(2,1)} async-done(((bf16[1,1280,256]{2,1,0:T(8,128)(2,1)}), bf16[1,5120,256]{2,1,0:T(8,128)(2,1)}) %all-gather.3.cloned.1.call-update) | async-done | bytes 2621456 | tf_op jit(solution)/shard_map/all_gather | solution.py:82
  67.1 2.6 bitcast_dynamic-update-slice_fusion.10
  69.7 52.5 %all-gather.5.cloned.1.call-done = bf16[1,256,5120]{2,1,0:T(8,128)(2,1)} async-done(((bf16[1,256,1280]{2,1,0:T(8,128)(2,1)}), bf16[1,256,5120]{2,1,0:T(8,128)(2,1)}) %all-gather.5.cloned.1.call-update) | async-done | bytes 2621456 | tf_op jit(solution)/shard_map/all_gather | solution.py:83
  122.2 3.2 convolution_convert_fusion.4
  128.5 14.6 %all-reduce.6.cloned.1.call-done = bf16[64,5120]{1,0:T(8,128)(2,1)} async-done(((bf16[64,5120]{1,0:T(8,128)(2,1)}), bf16[64,5120]{1,0:T(8,128)(2,1)}) %all-reduce.6.cloned.1.call-update) | async-done | bytes 655376 | tf_op jit(solution)/shard_map/psum | solution.py:117
  145.8 3.7 collective-permute-start
  150.7 13.2 %collective-permute-done = bf16[64,5120]{1,0:T(8,128)(2,1)S(1)} collective-permute-done((bf16[64,5120]{1,0:T(8,128)(2,1)S(1)}, bf16[64,5120]{1,0:T(8,128)(2,1)S(1)}, u32[]{:S(2)}, u32[]{:S(2)}) %collective-permute-start) | collective-permute-done | bytes 655392 | tf_op jit(solution)/shard_map/ppermute | solution.py:18
  172.6 16.8 %all-reduce.8.cloned.1.call-done = bf16[64,5120]{1,0:T(8,128)(2,1)} async-done(((bf16[64,5120]{1,0:T(8,128)(2,1)}), bf16[64,5120]{1,0:T(8,128)(2,1)}) %all-reduce.8.cloned.1.call-update) | async-done | bytes 655376 | tf_op jit(solution)/shard_map/psum | solution.py:117
  189.4 2.5 bitcast_dynamic-update-slice_fusion.4
  191.9 3.7 collective-permute-start.1
  195.6 2.2 constant_dynamic-slice_fusion.13
  197.8 12.1 %collective-permute-done.1 = bf16[64,5120]{1,0:T(8,128)(2,1)S(1)} collective-permute-done((bf16[64,5120]{1,0:T(8,128)(2,1)S(1)}, bf16[64,5120]{1,0:T(8,128)(2,1)S(1)}, u32[]{:S(2)}, u32[]{:S(2)}) %collective-permute-start.1) | collective-permute-done | bytes 655392 | tf_op jit(solution)/shard_map/ppermute | solution.py:18
  219.3 17.0 %all-reduce.10.cloned.1.call-done = bf16[64,5120]{1,0:T(8,128)(2,1)} async-done(((bf16[64,5120]{1,0:T(8,128)(2,1)}), bf16[64,5120]{1,0:T(8,128)(2,1)}) %all-reduce.10.cloned.1.call-update) | async-done | bytes 655376 | tf_op jit(solution)/shard_map/psum | solution.py:117
  236.2 3.1 bitcast_dynamic-update-slice_fusion.6
  239.3 2.4 fusion.32
  247.6 17.8 %all-reduce.12.cloned.1.call-done = bf16[64,5120]{1,0:T(8,128)(2,1)} async-done(((bf16[64,5120]{1,0:T(8,128)(2,1)}), bf16[64,5120]{1,0:T(8,128)(2,1)}) %all-reduce.12.cloned.1.call-update) | async-done | bytes 655376 | tf_op jit(solution)/shard_map/psum | solution.py:144
  271.8 16.1 %collective-permute-done.2 = bf16[64,5120]{1,0:T(8,128)(2,1)S(1)} collective-permute-done((bf16[64,5120]{1,0:T(8,128)(2,1)S(1)}, bf16[64,5120]{1,0:T(8,128)(2,1)S(1)}, u32[]{:S(2)}, u32[]{:S(2)}) %collective-permute-start.2) | collective-permute-done | bytes 655392 | tf_op jit(solution)/shard_map/ppermute | solution.py:18
  293.5 19.2 %all-reduce.14.cloned.1.call-done = bf16[64,5120]{1,0:T(8,128)(2,1)} async-done(((bf16[64,5120]{1,0:T(8,128)(2,1)}), bf16[64,5120]{1,0:T(8,128)(2,1)}) %all-reduce.14.cloned.1.call-update) | async-done | bytes 655376 | tf_op jit(solution)/shard_map/psum | solution.py:144
  318.6 16.3 %collective-permute-done.3 = bf16[64,5120]{1,0:T(8,128)(2,1)S(1)} collective-permute-done((bf16[64,5120]{1,0:T(8,128)(2,1)S(1)}, bf16[64,5120]{1,0:T(8,128)(2,1)S(1)}, u32[]{:S(2)}, u32[]{:S(2)}) %collective-permute-start.3) | collective-permute-done | bytes 655392 | tf_op jit(solution)/shard_map/ppermute | solution.py:18
  338.3 2.2 fusion.1
  340.5 2.7 pad_maximum_fusion
  344.5 12.9 %psum.47 = f32[]{:T(128)} all-reduce(f32[]{:T(128)} %convert_reduce_fusion), channel_id=1, replica_groups=mesh['groups'=2,'dp'=4,'section'=2,'tensor'=2] {'dp'}, use_global_device_ids=true, to_apply=%region_17.20 | all-reduce | flops 1 | bytes 8 | tf_op jit(solution)/shard_map/psum | solution.py:168
  357.4 80.2 %reduce-scatter.2.cloned.1.call-done = bf16[1280,512]{0,1:T(8,128)(2,1)} async-done(((bf16[5120,512]{0,1:T(8,128)(2,1)}), bf16[1280,512]{0,1:T(8,128)(2,1)}) %reduce-scatter.2.cloned.1.call-update) | async-done | bytes 1310736 | tf_op jit(solution)/shard_map/reduce_scatter | solution.py:156
  437.6 2.2 convert_divide_fusion
  (150 shorter events, 66.0 us)
Async XLA Ops:
  7.2 2.3 copy-start
  7.2 59.9 %all-gather.3.cloned.1.call-start = ((), (), s32[]{:S(2)}) async-start(), calls=%async_computation.1 | async-start | bytes 3276800 | tf_op jit(solution)/shard_map/all_gather | solution.py:82
  7.9 114.3 %all-gather.5.cloned.1.call-start = ((), (), s32[]{:S(2)}) async-start(), calls=%async_computation.2 | async-start | bytes 3276800 | tf_op jit(solution)/shard_map/all_gather | solution.py:83
  8.7 134.4 %all-reduce.6.cloned.1.call-start = ((), (), s32[]{:S(2)}) async-start(), calls=%async_computation.3 | async-start | bytes 1310720 | tf_op jit(solution)/shard_map/psum | solution.py:117
  11.2 2.4 copy-start.28
  11.2 3.0 copy-start.29
  14.8 52.3 %copy-start.26 = (f32[1,5120]{1,0:T(1,128)S(1)}, f32[1,5120]{1,0:T(1,128)}, u32[]{:S(2)}) copy-start(f32[1,5120]{1,0:T(1,128)} %param.19) | copy-start | bytes 61444
  125.4 64.0 %all-reduce.8.cloned.1.call-start = ((), (), s32[]{:S(2)}) async-start(), calls=%async_computation.4 | async-start | bytes 1310720 | tf_op jit(solution)/shard_map/psum | solution.py:117
  145.8 4.9 %copy-start.20 = (bf16[2,64,5120]{2,1,0:T(8,128)(2,1)}, bf16[2,64,5120]{2,1,0:T(8,128)(2,1)S(1)}, u32[]{:S(2)}) copy-start(bf16[2,64,5120]{2,1,0:T(8,128)(2,1)S(1)} %get-tuple-element.22) | copy-start | bytes 3932164
  145.8 18.1 %collective-permute-start = (bf16[64,5120]{1,0:T(8,128)(2,1)S(1)}, bf16[64,5120]{1,0:T(8,128)(2,1)S(1)}, u32[]{:S(2)}, u32[]{:S(2)}) collective-permute-start(bf16[64,5120]{1,0:T(8,128)(2,1)S(1)} %get-tuple-element.23), channel_id=1, source_target_pairs={{0,2},{1,3},{4,6},{5,7},{8,10},{9,11},{12,14},{13,15},{16,18},{17,... | collective-permute-start | bytes 1966088 | tf_op jit(solution)/shard_map/ppermute | solution.py:18
  150.7 14.6 %copy-start.8 = (bf16[1,5120,256]{2,1,0:T(8,128)(2,1)S(1)}, bf16[1,5120,256]{2,1,0:T(8,128)(2,1)}, u32[]{:S(2)}) copy-start(bf16[1,5120,256]{2,1,0:T(8,128)(2,1)} %all-gather.3.cloned.1.call-done) | copy-start | bytes 7864324
  168.5 67.7 %all-reduce.10.cloned.1.call-start = ((), (), s32[]{:S(2)}) async-start(), calls=%async_computation.5 | async-start | bytes 1310720 | tf_op jit(solution)/shard_map/psum | solution.py:117
  191.9 18.1 %collective-permute-start.1 = (bf16[64,5120]{1,0:T(8,128)(2,1)S(1)}, bf16[64,5120]{1,0:T(8,128)(2,1)S(1)}, u32[]{:S(2)}, u32[]{:S(2)}) collective-permute-start(bf16[64,5120]{1,0:T(8,128)(2,1)S(1)} %get-tuple-element.21), channel_id=1, source_target_pairs={{0,2},{1,3},{4,6},{5,7},{8,10},{9,11},{12,14},{13,15},{16,18},{17,... | collective-permute-start | bytes 1966088 | tf_op jit(solution)/shard_map/ppermute | solution.py:18
  195.6 14.5 %copy-start.15 = (bf16[16,8,5120]{2,1,0:T(8,128)(2,1)S(1)}, bf16[16,8,5120]{2,1,0:T(8,128)(2,1)}, u32[]{:S(2)}) copy-start(bf16[16,8,5120]{2,1,0:T(8,128)(2,1)} %copy-done.12) | copy-start | bytes 3932164
  195.6 14.5 %copy-start.25 = (bf16[1,64,5120]{2,1,0:T(8,128)(2,1)S(1)}, bf16[1,64,5120]{2,1,0:T(8,128)(2,1)}, u32[]{:S(2)}) copy-start(bf16[1,64,5120]{2,1,0:T(8,128)(2,1)} %constant_dynamic-slice_fusion.8) | copy-start | bytes 1966084
  215.4 50.0 %all-reduce.12.cloned.1.call-start = ((), (), s32[]{:S(2)}) async-start(), calls=%async_computation.6 | async-start | bytes 1310720 | tf_op jit(solution)/shard_map/psum | solution.py:144
  218.4 17.8 %copy-start.22 = (bf16[64,5120]{1,0:T(8,128)(2,1)S(1)}, bf16[64,5120]{1,0:T(8,128)(2,1)}, u32[]{:S(2)}) copy-start(bf16[64,5120]{1,0:T(8,128)(2,1)} %copy-done.21) | copy-start | bytes 1966084
  239.3 2.4 copy-start.5
  245.3 67.4 %all-reduce.14.cloned.1.call-start = ((), (), s32[]{:S(2)}) async-start(), calls=%async_computation.7 | async-start | bytes 1310720 | tf_op jit(solution)/shard_map/psum | solution.py:144
  265.4 2.1 copy-start.24
  269.2 18.8 %collective-permute-start.2 = (bf16[64,5120]{1,0:T(8,128)(2,1)S(1)}, bf16[64,5120]{1,0:T(8,128)(2,1)S(1)}, u32[]{:S(2)}, u32[]{:S(2)}) collective-permute-start(bf16[64,5120]{1,0:T(8,128)(2,1)S(1)} %fusion.46), channel_id=1, source_target_pairs={{2,0},{3,1},{6,4},{7,5},{10,8},{11,9},{14,12},{15,13},{18,16},{19,... | collective-permute-start | bytes 1966088 | tf_op jit(solution)/shard_map/ppermute | solution.py:18
  293.5 144.1 %reduce-scatter.2.cloned.1.call-start = ((), (), s32[]{:S(2)}) async-start(), calls=%async_computation.8 | async-start | bytes 6553600 | tf_op jit(solution)/shard_map/reduce_scatter | solution.py:156
  314.4 20.5 %copy-start.7 = (bf16[1,256,5120]{2,1,0:T(8,128)(2,1)S(1)}, bf16[1,256,5120]{2,1,0:T(8,128)(2,1)}, u32[]{:S(2)}) copy-start(bf16[1,256,5120]{2,1,0:T(8,128)(2,1)} %all-gather.5.cloned.1.call-done) | copy-start | bytes 7864324
  316.1 18.8 %collective-permute-start.3 = (bf16[64,5120]{1,0:T(8,128)(2,1)S(1)}, bf16[64,5120]{1,0:T(8,128)(2,1)S(1)}, u32[]{:S(2)}, u32[]{:S(2)}) collective-permute-start(bf16[64,5120]{1,0:T(8,128)(2,1)S(1)} %fusion.52), channel_id=1, source_target_pairs={{2,0},{3,1},{6,4},{7,5},{10,8},{11,9},{14,12},{15,13},{18,16},{19,... | collective-permute-start | bytes 1966088 | tf_op jit(solution)/shard_map/ppermute | solution.py:18
  (19 other events, 29.8 us)
Sparse Core Ops, SparseCore 0:
  9.6 57.4 all-gather.2
  68.6 53.4 all-gather.4
  125.5 17.5 all-reduce.5
  168.6 20.6 all-reduce.7
  215.5 20.6 all-reduce.9
  245.4 19.9 all-reduce.11
  293.6 19.0 all-reduce.13
  343.3 94.1 reduce-scatter.1
where the time goes:
time: 450 us; the launch traced here: 449 us
  waiting for transfers between devices  326 us (72%)
  local copies, waits for them, and re-layouts  32.9 us (7%)
  other arithmetic  32.2 us (7%)
  matrix products  19.3 us (4%)
  between operations  15.3 us (3%)
  blocking collectives  12.9 us (3%)
  starting transfers between devices  10.5 us (2%)
    reduce_scatter x1, waiting for transfers between devices, local(): lax.psum_scatter(jnp.concatenate([contract_first(flat_normed, flat_grad_v...  80.2 us
    ppermute x4, waiting for transfers between devices, from_behind(): return lax.ppermute(block, axis, route)  57.8 us
    all_gather x1, waiting for transfers between devices, local(): lax.all_gather(output_proj, 'dp', axis=2, tiled=True)  52.5 us
    all_gather x1, waiting for transfers between devices, local(): lax.all_gather(value_proj, 'dp', axis=1, tiled=True)  48.9 us
    psum x3, waiting for transfers between devices, local(): lax.psum(partial_out.astype(jnp.bfloat16), 'tensor').astype(jnp.float32)  48.4 us
    psum x2, waiting for transfers between devices, local(): lax.psum(partial_norm.astype(jnp.bfloat16), 'tensor').astype(jnp.float32)  37 us
    dynamic_update_slice x10, other arithmetic, put_slot(): lax.dynamic_update_index_in_dim(slot_store, jnp.where(active, new_value,...  14.3 us
    psum x1, blocking collectives, local(): token_total = lax.psum(local_count, 'dp')  12.9 us
  transfers between devices with their start and end apart: 12, of which 12 were waited for; matrix products, arithmetic and copies ran while one was open for 6% of the time, Pallas kernels for 0%

commit v1 on v0

--- a/solution.py
+++ b/solution.py
@@ -10,6 +10,11 @@
 loss_scale = 4096.0
 clip_high = math.log(1.28)
 clip_low = math.log(0.8)
+
+
+def summed_here(shard, axis):
+    parts = lax.all_gather(shard, axis)
+    return jnp.sum(parts, axis=0)
 
 
 def from_behind(block, axis, distance):
@@ -141,7 +146,7 @@
         projected = take_slot(store_projected, clamped)
         grad_projected = contract_last(upstream, w_second).astype(jnp.bfloat16)
         partial_norm = contract_last(grad_projected, w_first)
-        grad_normed = lax.psum(partial_norm.astype(jnp.bfloat16), "tensor").astype(jnp.float32)
+        grad_normed = summed_here(partial_norm.astype(jnp.bfloat16), "tensor").astype(jnp.float32)
         values, inverse, unused_normed = norm_forward(entering, norm_gain)
         grad_entering = (
             upstream.astype(jnp.float32) + norm_backward(values, inverse, norm_gain, grad_normed)

time: 450 us -> 435 us (0.967)
  waiting for transfers between devices: 326 us -> 307 us
    psum x2 -> x0, waiting for transfers between devices: 37 us -> none  [local(): lax.psum(partial_norm.astype(jnp.bfloat16), 'tensor').astype(jnp.float32)]
    all_gather x0 -> x2, waiting for transfers between devices: none -> 18.3 us  [summed_here(): parts = lax.all_gather(shard, axis)]
  transfers between devices with their start and end apart: 12 -> 12, of which waited for: 12 -> 12; matrix products, arithmetic and copies ran while one was open for 6% -> 7% of each run, Pallas kernels for 0% -> 0%
where the time goes in v1:
time: 435 us; the launch traced here: 433 us
  waiting for transfers between devices  307 us (71%)
  other arithmetic  35 us (8%)
  local copies, waits for them, and re-layouts  32.9 us (8%)
  matrix products  19.3 us (4%)
  between operations  15.3 us (4%)
  blocking collectives  13 us (3%)
  starting transfers between devices  10.5 us (2%)
    reduce_scatter x1, waiting for transfers between devices, local(): lax.psum_scatter(jnp.concatenate([contract_first(flat_normed, flat_grad_v...  80.2 us
    ppermute x4, waiting for transfers between devices, from_behind(): return lax.ppermute(block, axis, route)  57.7 us
    all_gather x1, waiting for transfers between devices, local(): lax.all_gather(output_proj, 'dp', axis=2, tiled=True)  52.5 us
    all_gather x1, waiting for transfers between devices, local(): lax.all_gather(value_proj, 'dp', axis=1, tiled=True)  48.9 us
    psum x3, waiting for transfers between devices, local(): lax.psum(partial_out.astype(jnp.bfloat16), 'tensor').astype(jnp.float32)  48.4 us
    all_gather x2, waiting for transfers between devices, summed_here(): parts = lax.all_gather(shard, axis)  18.3 us
    dynamic_update_slice x10, other arithmetic, put_slot(): lax.dynamic_update_index_in_dim(slot_store, jnp.where(active, new_value,...  14.3 us
    psum x1, blocking collectives, local(): token_total = lax.psum(local_count, 'dp')  13 us
  transfers between devices with their start and end apart: 12, of which 12 were waited for; matrix products, arithmetic and copies ran while one was open for 7% of the time, Pallas kernels for 0%

profile of v1, /device:TPU:0, one launch (start us, length us, event | category | flops | bytes accessed | tf_op | source)
XLA Modules:
  0.0 433.4 jit_solution(9999579876278382536)
XLA Ops:
  18.2 48.9 %all-gather.7.cloned.1.call-done = bf16[1,5120,256]{2,1,0:T(8,128)(2,1)} async-done(((bf16[1,1280,256]{2,1,0:T(8,128)(2,1)}), bf16[1,5120,256]{2,1,0:T(8,128)(2,1)}) %all-gather.7.cloned.1.call-update) | async-done | bytes 2621456 | tf_op jit(solution)/shard_map/all_gather | solution.py:87
  67.1 2.6 bitcast_dynamic-update-slice_fusion.10
  69.7 52.5 %all-gather.9.cloned.1.call-done = bf16[1,256,5120]{2,1,0:T(8,128)(2,1)} async-done(((bf16[1,256,1280]{2,1,0:T(8,128)(2,1)}), bf16[1,256,5120]{2,1,0:T(8,128)(2,1)}) %all-gather.9.cloned.1.call-update) | async-done | bytes 2621456 | tf_op jit(solution)/shard_map/all_gather | solution.py:88
  122.2 3.2 convolution_convert_fusion.4
  128.5 14.6 %all-reduce.4.cloned.1.call-done = bf16[64,5120]{1,0:T(8,128)(2,1)} async-done(((bf16[64,5120]{1,0:T(8,128)(2,1)}), bf16[64,5120]{1,0:T(8,128)(2,1)}) %all-reduce.4.cloned.1.call-update) | async-done | bytes 655376 | tf_op jit(solution)/shard_map/psum | solution.py:122
  145.8 3.7 collective-permute-start
  150.7 13.2 %collective-permute-done = bf16[64,5120]{1,0:T(8,128)(2,1)S(1)} collective-permute-done((bf16[64,5120]{1,0:T(8,128)(2,1)S(1)}, bf16[64,5120]{1,0:T(8,128)(2,1)S(1)}, u32[]{:S(2)}, u32[]{:S(2)}) %collective-permute-start) | collective-permute-done | bytes 655392 | tf_op jit(solution)/shard_map/ppermute | solution.py:23
  172.6 16.8 %all-reduce.6.cloned.1.call-done = bf16[64,5120]{1,0:T(8,128)(2,1)} async-done(((bf16[64,5120]{1,0:T(8,128)(2,1)}), bf16[64,5120]{1,0:T(8,128)(2,1)}) %all-reduce.6.cloned.1.call-update) | async-done | bytes 655376 | tf_op jit(solution)/shard_map/psum | solution.py:122
  189.4 2.5 bitcast_dynamic-update-slice_fusion.4
  191.9 3.7 collective-permute-start.1
  195.6 2.2 constant_dynamic-slice_fusion.13
  197.8 12.1 %collective-permute-done.1 = bf16[64,5120]{1,0:T(8,128)(2,1)S(1)} collective-permute-done((bf16[64,5120]{1,0:T(8,128)(2,1)S(1)}, bf16[64,5120]{1,0:T(8,128)(2,1)S(1)}, u32[]{:S(2)}, u32[]{:S(2)}) %collective-permute-start.1) | collective-permute-done | bytes 655392 | tf_op jit(solution)/shard_map/ppermute | solution.py:23
  219.3 17.0 %all-reduce.8.cloned.1.call-done = bf16[64,5120]{1,0:T(8,128)(2,1)} async-done(((bf16[64,5120]{1,0:T(8,128)(2,1)}), bf16[64,5120]{1,0:T(8,128)(2,1)}) %all-reduce.8.cloned.1.call-update) | async-done | bytes 655376 | tf_op jit(solution)/shard_map/psum | solution.py:122
  236.2 3.1 bitcast_dynamic-update-slice_fusion.6
  239.3 2.4 fusion.32
  247.7 8.4 %all-gather.11.cloned.1.call-done = bf16[128,5120]{1,0:T(8,128)(2,1)} async-done(((bf16[64,5120]{1,0:T(8,128)(2,1)}), bf16[128,5120]{1,0:T(8,128)(2,1)}) %all-gather.11.cloned.1.call-update) | async-done | bytes 1310736 | tf_op jit(solution)/shard_map/all_gather | solution.py:16
  263.9 16.1 %collective-permute-done.2 = bf16[64,5120]{1,0:T(8,128)(2,1)S(1)} collective-permute-done((bf16[64,5120]{1,0:T(8,128)(2,1)S(1)}, bf16[64,5120]{1,0:T(8,128)(2,1)S(1)}, u32[]{:S(2)}, u32[]{:S(2)}) %collective-permute-start.2) | collective-permute-done | bytes 655392 | tf_op jit(solution)/shard_map/ppermute | solution.py:23
  285.6 9.8 %all-gather.13.cloned.1.call-done = bf16[128,5120]{1,0:T(8,128)(2,1)} async-done(((bf16[64,5120]{1,0:T(8,128)(2,1)}), bf16[128,5120]{1,0:T(8,128)(2,1)}) %all-gather.13.cloned.1.call-update) | async-done | bytes 1310736 | tf_op jit(solution)/shard_map/all_gather | solution.py:16
  302.7 16.3 %collective-permute-done.3 = bf16[64,5120]{1,0:T(8,128)(2,1)S(1)} collective-permute-done((bf16[64,5120]{1,0:T(8,128)(2,1)S(1)}, bf16[64,5120]{1,0:T(8,128)(2,1)S(1)}, u32[]{:S(2)}, u32[]{:S(2)}) %collective-permute-start.3) | collective-permute-done | bytes 655392 | tf_op jit(solution)/shard_map/ppermute | solution.py:23
  322.4 2.2 fusion.1
  324.6 2.7 pad_maximum_fusion
  328.6 13.0 %psum.31 = f32[]{:T(128)} all-reduce(f32[]{:T(128)} %convert_reduce_fusion), channel_id=1, replica_groups=mesh['groups'=2,'dp'=4,'section'=2,'tensor'=2] {'dp'}, use_global_device_ids=true, to_apply=%region_17.20 | all-reduce | flops 1 | bytes 8 | tf_op jit(solution)/shard_map/psum | solution.py:173
  341.6 80.2 %reduce-scatter.2.cloned.1.call-done = bf16[1280,512]{0,1:T(8,128)(2,1)} async-done(((bf16[5120,512]{0,1:T(8,128)(2,1)}), bf16[1280,512]{0,1:T(8,128)(2,1)}) %reduce-scatter.2.cloned.1.call-update) | async-done | bytes 1310736 | tf_op jit(solution)/shard_map/reduce_scatter | solution.py:161
  421.7 2.2 convert_divide_fusion
  (152 shorter events, 68.8 us)
Async XLA Ops:
  7.2 2.3 copy-start
  7.2 59.9 %all-gather.7.cloned.1.call-start = ((), (), s32[]{:S(2)}) async-start(), calls=%async_computation.1 | async-start | bytes 3276800 | tf_op jit(solution)/shard_map/all_gather | solution.py:87
  7.9 114.3 %all-gather.9.cloned.1.call-start = ((), (), s32[]{:S(2)}) async-start(), calls=%async_computation.2 | async-start | bytes 3276800 | tf_op jit(solution)/shard_map/all_gather | solution.py:88
  8.7 134.4 %all-reduce.4.cloned.1.call-start = ((), (), s32[]{:S(2)}) async-start(), calls=%async_computation.3 | async-start | bytes 1310720 | tf_op jit(solution)/shard_map/psum | solution.py:122
  11.2 2.4 copy-start.28
  11.2 3.0 copy-start.29
  14.8 52.3 %copy-start.26 = (f32[1,5120]{1,0:T(1,128)S(1)}, f32[1,5120]{1,0:T(1,128)}, u32[]{:S(2)}) copy-start(f32[1,5120]{1,0:T(1,128)} %param.19) | copy-start | bytes 61444
  125.4 64.0 %all-reduce.6.cloned.1.call-start = ((), (), s32[]{:S(2)}) async-start(), calls=%async_computation.4 | async-start | bytes 1310720 | tf_op jit(solution)/shard_map/psum | solution.py:122
  145.8 4.9 %copy-start.20 = (bf16[2,64,5120]{2,1,0:T(8,128)(2,1)}, bf16[2,64,5120]{2,1,0:T(8,128)(2,1)S(1)}, u32[]{:S(2)}) copy-start(bf16[2,64,5120]{2,1,0:T(8,128)(2,1)S(1)} %get-tuple-element.22) | copy-start | bytes 3932164
  145.8 18.1 %collective-permute-start = (bf16[64,5120]{1,0:T(8,128)(2,1)S(1)}, bf16[64,5120]{1,0:T(8,128)(2,1)S(1)}, u32[]{:S(2)}, u32[]{:S(2)}) collective-permute-start(bf16[64,5120]{1,0:T(8,128)(2,1)S(1)} %get-tuple-element.23), channel_id=1, source_target_pairs={{0,2},{1,3},{4,6},{5,7},{8,10},{9,11},{12,14},{13,15},{16,18},{17,... | collective-permute-start | bytes 1966088 | tf_op jit(solution)/shard_map/ppermute | solution.py:23
  150.7 14.6 %copy-start.8 = (bf16[1,5120,256]{2,1,0:T(8,128)(2,1)S(1)}, bf16[1,5120,256]{2,1,0:T(8,128)(2,1)}, u32[]{:S(2)}) copy-start(bf16[1,5120,256]{2,1,0:T(8,128)(2,1)} %all-gather.7.cloned.1.call-done) | copy-start | bytes 7864324
  168.5 67.7 %all-reduce.8.cloned.1.call-start = ((), (), s32[]{:S(2)}) async-start(), calls=%async_computation.5 | async-start | bytes 1310720 | tf_op jit(solution)/shard_map/psum | solution.py:122
  191.9 18.1 %collective-permute-start.1 = (bf16[64,5120]{1,0:T(8,128)(2,1)S(1)}, bf16[64,5120]{1,0:T(8,128)(2,1)S(1)}, u32[]{:S(2)}, u32[]{:S(2)}) collective-permute-start(bf16[64,5120]{1,0:T(8,128)(2,1)S(1)} %get-tuple-element.21), channel_id=1, source_target_pairs={{0,2},{1,3},{4,6},{5,7},{8,10},{9,11},{12,14},{13,15},{16,18},{17,... | collective-permute-start | bytes 1966088 | tf_op jit(solution)/shard_map/ppermute | solution.py:23
  195.6 14.5 %copy-start.15 = (bf16[16,8,5120]{2,1,0:T(8,128)(2,1)S(1)}, bf16[16,8,5120]{2,1,0:T(8,128)(2,1)}, u32[]{:S(2)}) copy-start(bf16[16,8,5120]{2,1,0:T(8,128)(2,1)} %copy-done.12) | copy-start | bytes 3932164
  195.6 14.5 %copy-start.25 = (bf16[1,64,5120]{2,1,0:T(8,128)(2,1)S(1)}, bf16[1,64,5120]{2,1,0:T(8,128)(2,1)}, u32[]{:S(2)}) copy-start(bf16[1,64,5120]{2,1,0:T(8,128)(2,1)} %constant_dynamic-slice_fusion.8) | copy-start | bytes 1966084
  210.1 2.0 copy-start.9
  215.4 40.7 %all-gather.11.cloned.1.call-start = ((), (), s32[]{:S(2)}) async-start(), calls=%async_computation.7 | async-start | bytes 1966080 | tf_op jit(solution)/shard_map/all_gather | solution.py:16
  218.4 17.8 %copy-start.22 = (bf16[64,5120]{1,0:T(8,128)(2,1)S(1)}, bf16[64,5120]{1,0:T(8,128)(2,1)}, u32[]{:S(2)}) copy-start(bf16[64,5120]{1,0:T(8,128)(2,1)} %copy-done.21) | copy-start | bytes 1966084
  239.3 2.4 copy-start.5
  245.3 50.1 %all-gather.13.cloned.1.call-start = ((), (), s32[]{:S(2)}) async-start(), calls=%async_computation.8 | async-start | bytes 1966080 | tf_op jit(solution)/shard_map/all_gather | solution.py:16
  261.3 18.8 %collective-permute-start.2 = (bf16[64,5120]{1,0:T(8,128)(2,1)S(1)}, bf16[64,5120]{1,0:T(8,128)(2,1)S(1)}, u32[]{:S(2)}, u32[]{:S(2)}) collective-permute-start(bf16[64,5120]{1,0:T(8,128)(2,1)S(1)} %fusion.46), channel_id=1, source_target_pairs={{2,0},{3,1},{6,4},{7,5},{10,8},{11,9},{14,12},{15,13},{18,16},{19,... | collective-permute-start | bytes 1966088 | tf_op jit(solution)/shard_map/ppermute | solution.py:23
  285.5 136.2 %reduce-scatter.2.cloned.1.call-start = ((), (), s32[]{:S(2)}) async-start(), calls=%async_computation.6 | async-start | bytes 6553600 | tf_op jit(solution)/shard_map/reduce_scatter | solution.py:161
  298.5 20.5 %copy-start.7 = (bf16[1,256,5120]{2,1,0:T(8,128)(2,1)S(1)}, bf16[1,256,5120]{2,1,0:T(8,128)(2,1)}, u32[]{:S(2)}) copy-start(bf16[1,256,5120]{2,1,0:T(8,128)(2,1)} %all-gather.9.cloned.1.call-done) | copy-start | bytes 7864324
  300.3 18.8 %collective-permute-start.3 = (bf16[64,5120]{1,0:T(8,128)(2,1)S(1)}, bf16[64,5120]{1,0:T(8,128)(2,1)S(1)}, u32[]{:S(2)}, u32[]{:S(2)}) collective-permute-start(bf16[64,5120]{1,0:T(8,128)(2,1)S(1)} %fusion.52), channel_id=1, source_target_pairs={{2,0},{3,1},{6,4},{7,5},{10,8},{11,9},{14,12},{15,13},{18,16},{19,... | collective-permute-start | bytes 1966088 | tf_op jit(solution)/shard_map/ppermute | solution.py:23
  (19 other events, 29.4 us)
Sparse Core Ops, SparseCore 0:
  9.6 57.4 all-gather.6
  68.6 53.4 all-gather.8
  125.5 17.5 all-reduce.3
  168.6 20.6 all-reduce.5
  215.5 20.6 all-reduce.7
  245.5 10.6 all-gather.10
  285.6 9.7 all-gather.12
  327.4 94.2 reduce-scatter.1
